TPU v7x, 32 devices: a whole 2x2x4 slice. The times are simulated.
32 devices in a mesh: cell: 16 (over z, y, x), gene: 2 (over core).
Axes of the slice: x: 2, y: 2, z: 4, core: 2. Of those that a mesh axis runs over, the one named last changes fastest.
Arguments:
- tiles: bfloat16 [2, 1024, 128, 128], P('gene', 'cell'), may hold values from -8 to 8
- tile_row: int32 [2, 1024], P('gene', 'cell'), may hold values from 0 to 7, as said below
- tile_col: int32 [2, 1024], P('gene', 'cell'), may hold values from 0 to 15
- tile_count: int32 [2, 16], P('gene', 'cell'), may hold values from 1 to 64, as said below
- start_basis: bfloat16 [64, 4096], P(None, 'gene'), may hold values from -0.09375 to 0.09375
Outputs:
- basis: bfloat16 [64, 16384], P(None, 'cell')
- loadings: float32 [64, 4096], P(None, ('gene', 'cell'))
Inputs may be any that keep to these rules, and one draw needn't show every extreme that they name: `tile_row`: tile row of each slot, within 0 to 7; the slots of one device name distinct (row, column) pairs. `tile_count`: slots in use; for each index of gene some device uses all 64.
All inputs are finite; a program needn't handle non-finite values.
Results may differ from a plain program's by a relative error of at most 0.018.
Values may be sent and summed in bfloat16 or wider, within the bound.
No kernel may reach another device: no remote copies, remote signals or barrier semaphores. Data moves between devices by JAX's collectives and lax.ppermute only.
A program may use at most 64 MiB of HBM per device.

v0:
```python
import jax
import jax.numpy as jnp
from jax import lax
from jax.sharding import PartitionSpec as P

ROW_BLOCKS = 8


def solve_lower(lower, right):
    return lax.linalg.triangular_solve(lower, right, left_side=True, lower=True)


def gram_of(scores):
    return jnp.dot(
        scores, scores.T, precision=lax.Precision.HIGHEST, preferred_element_type=jnp.float32
    )


def orthonormal(scores, first_total):
    first = first_total(gram_of(scores))
    lower_one = jnp.linalg.cholesky(first)
    return solve_lower(lower_one, scores)


def local(tiles, tile_row, tile_col, tile_count, start_basis):
    blocks_local = tiles[0]
    slot_count = blocks_local.shape[0]
    tile_size = blocks_local.shape[-1]
    width = start_basis.shape[0]
    gene_dev = start_basis.shape[1]
    gene_blocks = gene_dev // tile_size
    row_blocks = ROW_BLOCKS
    cell_dev = row_blocks * tile_size
    row_index = tile_row[0]
    col_index = tile_col[0]
    live = jnp.arange(slot_count) < tile_count[0, 0]
    row_target = jnp.where(live, row_index, row_blocks)
    col_target = jnp.where(live, col_index, gene_blocks)

    def first_total(gram):
        return lax.psum(gram, ("cell", "gene"))

    def merge_halves(partial_scores):
        return lax.psum_scatter(partial_scores, "gene", scatter_dimension=1, tiled=True)

    def scores_of(basis):
        picked = jnp.take(basis.reshape(width, gene_blocks, tile_size), col_index, axis=1)
        products = jnp.einsum(
            "ksg,srg->skr", picked, blocks_local, preferred_element_type=jnp.float32
        )
        summed = jax.ops.segment_sum(products, row_target, num_segments=row_blocks + 1)[:row_blocks]
        return merge_halves(jnp.transpose(summed, (1, 0, 2)).reshape(width, cell_dev))

    def loadings_of(ortho_half):
        picked = jnp.take(ortho_half.reshape(width, row_blocks, tile_size), row_index, axis=1)
        products = jnp.einsum(
            "ksr,srg->skg", picked, blocks_local, preferred_element_type=jnp.float32
        )
        summed = jax.ops.segment_sum(products, col_target, num_segments=gene_blocks + 1)[
            :gene_blocks
        ]
        return jnp.transpose(summed, (1, 0, 2)).reshape(width, gene_dev)

    ortho = orthonormal(scores_of(start_basis), first_total)
    ortho_half = ortho.astype(jnp.bfloat16)
    ortho_rows = lax.all_gather(ortho_half, "gene", axis=1, tiled=True)
    partial_value = loadings_of(ortho_rows)
    next_basis = lax.psum(partial_value, "cell").astype(jnp.bfloat16)
    ortho_two = orthonormal(scores_of(next_basis), first_total)
    scale = jnp.sqrt(jnp.float32(lax.axis_size("cell") * cell_dev))
    ortho_two_half = ortho_two.astype(jnp.bfloat16)
    basis_piece = (ortho_two * scale).astype(jnp.bfloat16)
    final_rows, basis = (
        lax.all_gather(ortho_two_half, "gene", axis=1, tiled=True),
        lax.all_gather(basis_piece, "gene", axis=1, tiled=True),
    )
    loadings = lax.psum_scatter(loadings_of(final_rows), "cell", scatter_dimension=1, tiled=True)
    return (basis, loadings)


def solution(mesh):
    return jax.shard_map(
        local,
        mesh=mesh,
        in_specs=(
            P("gene", "cell", None, None),
            P("gene", "cell"),
            P("gene", "cell"),
            P("gene", "cell"),
            P(None, "gene"),
        ),
        out_specs=(P(None, "cell"), P(None, ("gene", "cell"))),
        check_vma=False,
    )
```

profile of v0, /device:TPU:0, one launch (start us, length us, event | category | flops | bytes accessed | tf_op | source)
XLA Modules:
  0.0 349.9 jit_solution(15291023441210544630)
XLA Ops:
  7.2 0.0 copy-start
  7.2 0.0 copy-start.1
  7.2 0.0 copy-start.2
  7.2 0.0 reduce-scatter.4.cloned.1.call-start
  7.2 0.8 compare_select_fusion
  8.0 0.7 compare_and_fusion
  8.7 1.0 copy_bitcast_fusion.5
  10.4 0.7 gather_fusion
  11.1 0.0 copy-done.1
  11.2 0.0 copy-done.2
  11.2 0.0 copy-done
  11.2 2.9 fusion.6
  14.1 7.1 %scatter_fusion = f32[9,64,128]{2,1,0:T(8,128)S(1)} fusion(f32[9,64,128]{2,1,0:T(8,128)S(1)} %broadcast.69.clone, s32[64]{0:T(128)S(1)} %get-tuple-element.8, f32[64,64,128]{2,1,0:T(8,128)} %fusion.6), kind=kCustom, calls=%fused_computation.4 | custom fusion | flops 524288 | bytes 6291712 | tf_op jit(solution)/shard_map/scatter-add | solution.py:51
  21.2 0.7 copy_bitcast_fusion.3
  21.9 0.0 reduce-scatter.4.cloned.1.call-update
  21.9 0.0 reduce-scatter.6.cloned.1.call-start
  22.0 10.5 %reduce-scatter.4.cloned.1.call-done = f32[64,512]{1,0:T(8,128)} async-done(((f32[64,1024]{1,0:T(8,128)}), f32[64,512]{1,0:T(8,128)}) %reduce-scatter.4.cloned.1.call-update) | async-done | bytes 131088 | tf_op jit(solution)/shard_map/reduce_scatter | solution.py:44
  32.5 1.2 fusion.40
  33.8 40.5 %psum.21 = f32[64,64]{0,1:T(8,128)S(1)} all-reduce(f32[64,64]{0,1:T(8,128)S(1)} %fusion.40), channel_id=1, replica_groups=mesh['cell'=16,'gene'=2] {'cell','gene'}, use_global_device_ids=true, to_apply=%region_2.4 | all-reduce | flops 4096 | bytes 32768 | tf_op jit(solution)/shard_map/psum | solution.py:41
  74.3 0.1 copy.20
  74.4 5.8 %cholesky.44 = f32[64,64]{1,0:T(8,128)S(1)} custom-call(f32[64,64]{1,0:T(8,128)S(1)} %fusion.30), custom_call_target="Cholesky" | custom-call | tf_op jit(solution)/shard_map/jit(cholesky)/cholesky | solution.py:21
  80.3 0.6 compare_reduce_fusion.1
  80.9 0.7 fusion.24
  81.6 4.9 %custom-call.6 = f32[1,64,64]{1,2,0:T(8,128)S(1)} custom-call(f32[1,64,64]{2,1,0:T(8,128)S(1)} %fusion.24), custom_call_target="InvertDiagBlocksLowerTriangular" | custom-call | tf_op jit(solution)/shard_map/triangular_solve/custom-call.0 | solution.py:10
  86.5 1.2 convolution_convert_fusion
  87.7 1.9 all_gather.9
  89.7 0.7 gather_fusion.1
  90.4 2.1 fusion.4
  92.6 7.1 %scatter_fusion.1 = f32[17,64,128]{2,1,0:T(8,128)S(1)} fusion(f32[17,64,128]{2,1,0:T(8,128)S(1)} %broadcast.70.clone, s32[64]{0:T(128)S(1)} %get-tuple-element.9, f32[64,64,128]{2,1,0:T(8,128)} %fusion.4), kind=kCustom, calls=%fused_computation.5 | custom fusion | flops 524288 | bytes 6291712 | tf_op jit(solution)/shard_map/scatter-add | solution.py:59
  99.7 81.7 %all-reduce.1 = bf16[64,2048]{1,0:T(8,128)(2,1)S(1)} all-reduce(f32[64,2048]{1,0:T(8,128)S(1)} %copy_bitcast_fusion.1), channel_id=1, replica_groups=mesh['cell'=16,'gene'=2] {'cell'}, use_global_device_ids=true, to_apply=%region_6.11 | all-reduce | flops 131072 | bytes 786432 | tf_op jit(solution)/shard_map/psum | solution.py:68
  181.3 0.1 copy_bitcast_fusion.4
  181.4 0.8 gather_fusion.2
  182.2 2.9 fusion.2
  185.1 7.1 %scatter_fusion.2 = f32[9,64,128]{2,1,0:T(8,128)S(1)} fusion(f32[9,64,128]{2,1,0:T(8,128)S(1)} %broadcast.69, s32[64]{0:T(128)S(1)} %get-tuple-element.8, f32[64,64,128]{2,1,0:T(8,128)} %fusion.2), kind=kCustom, calls=%fused_computation.6 | custom fusion | flops 524288 | bytes 6291712 | tf_op jit(solution)/shard_map/scatter-add | solution.py:51
  192.2 0.7 copy_bitcast_fusion.2
  192.9 0.0 reduce-scatter.6.cloned.1.call-update
  192.9 0.0 reduce-scatter.8.cloned.1.call-start
  192.9 4.2 %reduce-scatter.6.cloned.1.call-done = f32[64,512]{1,0:T(8,128)} async-done(((f32[64,1024]{1,0:T(8,128)}), f32[64,512]{1,0:T(8,128)}) %reduce-scatter.6.cloned.1.call-update) | async-done | bytes 131088 | tf_op jit(solution)/shard_map/reduce_scatter | solution.py:44
  197.1 1.2 fusion.41
  198.4 40.8 %psum.23 = f32[64,64]{0,1:T(8,128)S(1)} all-reduce(f32[64,64]{0,1:T(8,128)S(1)} %fusion.41), channel_id=1, replica_groups=mesh['cell'=16,'gene'=2] {'cell','gene'}, use_global_device_ids=true, to_apply=%region_9.14 | all-reduce | flops 4096 | bytes 32768 | tf_op jit(solution)/shard_map/psum | solution.py:41
  239.1 0.1 copy.26
  239.2 5.8 %cholesky.55 = f32[64,64]{1,0:T(8,128)S(1)} custom-call(f32[64,64]{1,0:T(8,128)S(1)} %fusion.28), custom_call_target="Cholesky" | custom-call | tf_op jit(solution)/shard_map/jit(cholesky)/cholesky | solution.py:21
  245.1 0.6 compare_reduce_fusion
  245.8 0.7 fusion.25
  246.4 4.9 %custom-call.7 = f32[1,64,64]{1,2,0:T(8,128)S(1)} custom-call(f32[1,64,64]{2,1,0:T(8,128)S(1)} %fusion.25), custom_call_target="InvertDiagBlocksLowerTriangular" | custom-call | tf_op jit(solution)/shard_map/triangular_solve/custom-call.0 | solution.py:10
  251.3 1.2 fusion.39
  252.6 1.9 all_gather.11
  254.5 0.7 gather_fusion.3
  255.2 2.1 fusion
  257.4 7.1 %scatter_fusion.3 = f32[17,64,128]{2,1,0:T(8,128)S(1)} fusion(f32[17,64,128]{2,1,0:T(8,128)S(1)} %broadcast.70, s32[64]{0:T(128)S(1)} %get-tuple-element.9, f32[64,64,128]{2,1,0:T(8,128)} %fusion), kind=kCustom, calls=%fused_computation.7 | custom fusion | flops 524288 | bytes 6291712 | tf_op jit(solution)/shard_map/scatter-add | solution.py:59
  264.4 0.8 copy_bitcast_fusion
  265.3 0.0 reduce-scatter.8.cloned.1.call-update
  265.3 1.9 all_gather.10
  267.2 75.5 %reduce-scatter.8.cloned.1.call-done = f32[64,128]{1,0:T(8,128)} async-done(((f32[64,2048]{1,0:T(8,128)}), f32[64,128]{1,0:T(8,128)}) %reduce-scatter.8.cloned.1.call-update) | async-done | bytes 32784 | tf_op jit(solution)/shard_map/reduce_scatter | solution.py:77
  342.7 0.7 copy.55
  (16 shorter events, 0.3 us)
Async XLA Ops:
  7.2 4.0 %copy-start = (bf16[1,64,128,128]{3,2,1,0:T(8,128)(2,1)S(1)}, bf16[1,64,128,128]{3,2,1,0:T(8,128)(2,1)}, u32[]{:S(2)}) copy-start(bf16[1,64,128,128]{3,2,1,0:T(8,128)(2,1)} %param.12) | copy-start | bytes 6291460
  7.2 4.0 %copy-start.1 = (s32[1,64]{1,0:T(1,128)S(1)}, s32[1,64]{1,0:T(1,128)}, u32[]{:S(2)}) copy-start(s32[1,64]{1,0:T(1,128)} %param.14) | copy-start | bytes 772
  7.2 4.0 %copy-start.2 = (s32[1,64]{1,0:T(1,128)S(1)}, s32[1,64]{1,0:T(1,128)}, u32[]{:S(2)}) copy-start(s32[1,64]{1,0:T(1,128)} %param.13) | copy-start | bytes 772
  7.2 25.3 %reduce-scatter.4.cloned.1.call-start = ((), (), s32[]{:S(2)}) async-start(), calls=%async_computation.3 | async-start | bytes 393216 | tf_op jit(solution)/shard_map/reduce_scatter | solution.py:44
  21.9 175.2 %reduce-scatter.6.cloned.1.call-start = ((), (), s32[]{:S(2)}) async-start(), calls=%async_computation.4 | async-start | bytes 393216 | tf_op jit(solution)/shard_map/reduce_scatter | solution.py:44
  192.9 149.8 %reduce-scatter.8.cloned.1.call-start = ((), (), s32[]{:S(2)}) async-start(), calls=%async_computation.5 | async-start | bytes 557056 | tf_op jit(solution)/shard_map/reduce_scatter | solution.py:77
Sparse Core Ops, SparseCore 0:
  22.0 10.4 reduce-scatter.3
  193.0 4.0 reduce-scatter.5
  265.4 77.2 reduce-scatter.7
where the time goes:
time: 351 us; the launch traced here: 350 us
  blocking collectives  169 us (48%)
  waiting for transfers between devices  90.3 us (26%)
  other arithmetic  53.9 us (15%)
  matrix products  14.9 us (4%)
  between operations  14.7 us (4%)
  local copies, waits for them, and re-layouts  7.35 us (2%)
    psum x1, blocking collectives, local(): next_basis = lax.psum(partial_value, 'cell').astype(jnp.bfloat16)  81.7 us
    psum x2, blocking collectives, first_total(): return lax.psum(gram, ('cell', 'gene'))  81.3 us
    reduce_scatter x1, waiting for transfers between devices, local(): lax.psum_scatter(loadings_of(final_rows), 'cell', scatter_dimension=1, ti...  75.5 us
    reduce_scatter x2, waiting for transfers between devices, merge_halves(): lax.psum_scatter(partial_scores, 'gene', scatter_dimension=1, tiled=True)  14.7 us
    scatter-add x2, other arithmetic, scores_of(): jax.ops.segment_sum(products, row_target, num_segments=row_blocks + 1)  14.1 us
    scatter-add x2, other arithmetic, loadings_of(): jax.ops.segment_sum(products, col_target, num_segments=gene_blocks + 1)  14.1 us
    another operation x6, other arithmetic, orthonormal(): lower_one = jnp.linalg.cholesky(first)  13 us
    another operation x4, other arithmetic, solve_lower(): return lax.linalg.triangular_solve(lower, right, left_side=True, lower=True)  11.1 us
  transfers between devices with their start and end apart: 3, of which 3 were waited for; matrix products, arithmetic and copies ran while one was open for 0% of the time, Pallas kernels for 0%

commit v1 on v0

--- a/solution.py
+++ b/solution.py
@@ -38,7 +38,12 @@
     col_target = jnp.where(live, col_index, gene_blocks)
 
     def first_total(gram):
-        return lax.psum(gram, ("cell", "gene"))
+
+        def recast_the_side(t0):
+            res = lax.all_gather(t0, ("cell", "gene")).sum(axis=0)
+            return res
+
+        return recast_the_side(gram)
 
     def merge_halves(partial_scores):
         return lax.psum_scatter(partial_scores, "gene", scatter_dimension=1, tiled=True)

time: 351 us -> 351 us (level)
  blocking collectives: 169 us -> 173 us
    all_gather x0 -> x2, blocking collectives: none -> 89.3 us  [recast_the_side(): res = lax.all_gather(t0, ('cell', 'gene')).sum(axis=0)]
    psum x2 -> x0, blocking collectives: 81.3 us -> none  [first_total(): return lax.psum(gram, ('cell', 'gene'))]
    psum x1, blocking collectives: 81.7 us -> 77.5 us  [local(): next_basis = lax.psum(partial_value, 'cell').astype(jnp.bfloat16)]
    reduce_scatter x1, waiting for transfers between devices: 75.5 us -> 71.8 us  [local(): lax.psum_scatter(loadings_of(final_rows), 'cell', scatter_dimension=1, ti...]
where the time goes in v1:
time: 351 us; the launch traced here: 350 us
  blocking collectives  173 us (49%)
  waiting for transfers between devices  88.3 us (25%)
  other arithmetic  54 us (15%)
  between operations  14.7 us (4%)
  matrix products  13.2 us (4%)
  local copies, waits for them, and re-layouts  7.38 us (2%)
    all_gather x2, blocking collectives, recast_the_side(): res = lax.all_gather(t0, ('cell', 'gene')).sum(axis=0)  89.3 us
    psum x1, blocking collectives, local(): next_basis = lax.psum(partial_value, 'cell').astype(jnp.bfloat16)  77.5 us
    reduce_scatter x1, waiting for transfers between devices, local(): lax.psum_scatter(loadings_of(final_rows), 'cell', scatter_dimension=1, ti...  71.8 us
    reduce_scatter x2, waiting for transfers between devices, merge_halves(): lax.psum_scatter(partial_scores, 'gene', scatter_dimension=1, tiled=True)  16.4 us
    scatter-add x2, other arithmetic, scores_of(): jax.ops.segment_sum(products, row_target, num_segments=row_blocks + 1)  14.1 us
    scatter-add x2, other arithmetic, loadings_of(): jax.ops.segment_sum(products, col_target, num_segments=gene_blocks + 1)  14.1 us
    another operation x6, other arithmetic, orthonormal(): lower_one = jnp.linalg.cholesky(first)  13 us
    another operation x4, other arithmetic, solve_lower(): return lax.linalg.triangular_solve(lower, right, left_side=True, lower=True)  11.1 us
  transfers between devices with their start and end apart: 3, of which 3 were waited for; matrix products, arithmetic and copies ran while one was open for 0% of the time, Pallas kernels for 0%

profile of v1, /device:TPU:0, one launch (start us, length us, event | category | flops | bytes accessed | tf_op | source)
XLA Modules:
  0.0 350.2 jit_solution(892566930034612232)
XLA Ops:
  7.2 0.0 copy-start
  7.2 0.0 copy-start.3
  7.2 0.0 copy-start.4
  7.2 0.0 reduce-scatter.4.cloned.1.call-start
  7.2 0.8 compare_select_fusion
  8.0 0.7 compare_and_fusion
  8.7 1.0 copy_bitcast_fusion.5
  10.4 0.7 gather_fusion
  11.1 0.0 copy-done.3
  11.2 0.0 copy-done.4
  11.2 0.0 copy-done
  11.2 2.9 fusion.6
  14.1 7.1 %scatter_fusion = f32[9,64,128]{2,1,0:T(8,128)S(1)} fusion(f32[9,64,128]{2,1,0:T(8,128)S(1)} %broadcast.69.clone, s32[64]{0:T(128)S(1)} %get-tuple-element.8, f32[64,64,128]{2,1,0:T(8,128)} %fusion.6), kind=kCustom, calls=%fused_computation.4 | custom fusion | flops 524288 | bytes 6291712 | tf_op jit(solution)/shard_map/scatter-add | solution.py:56
  21.2 0.7 copy_bitcast_fusion.3
  21.9 0.0 reduce-scatter.4.cloned.1.call-update
  21.9 0.0 reduce-scatter.6.cloned.1.call-start
  22.0 10.5 %reduce-scatter.4.cloned.1.call-done = f32[64,512]{1,0:T(8,128)} async-done(((f32[64,1024]{1,0:T(8,128)}), f32[64,512]{1,0:T(8,128)}) %reduce-scatter.4.cloned.1.call-update) | async-done | bytes 131088 | tf_op jit(solution)/shard_map/reduce_scatter | solution.py:49
  32.5 0.0 copy-start.1
  32.5 1.3 fusion.40
  33.8 44.7 %all-gather = f32[2048,64]{1,0:T(8,128)S(1)} all-gather(f32[64,64]{1,0:T(8,128)S(1)} %fusion.40), channel_id=2, replica_groups=mesh['cell'=16,'gene'=2] {'cell','gene'}, dimensions={0}, use_global_device_ids=true | all-gather | bytes 540672 | tf_op jit(solution)/shard_map/all_gather | solution.py:43
  78.5 0.1 reduce_sum.18
  78.6 0.1 copy.25
  78.7 5.8 %cholesky.44 = f32[64,64]{1,0:T(8,128)S(1)} custom-call(f32[64,64]{1,0:T(8,128)S(1)} %fusion.30), custom_call_target="Cholesky" | custom-call | tf_op jit(solution)/shard_map/jit(cholesky)/cholesky | solution.py:21
  84.6 0.6 compare_reduce_fusion.1
  85.2 0.7 fusion.24
  85.9 4.9 %custom-call.6 = f32[1,64,64]{1,2,0:T(8,128)S(1)} custom-call(f32[1,64,64]{2,1,0:T(8,128)S(1)} %fusion.24), custom_call_target="InvertDiagBlocksLowerTriangular" | custom-call | tf_op jit(solution)/shard_map/triangular_solve/custom-call.0 | solution.py:10
  90.8 0.0 copy-done.1
  90.8 0.3 convolution_convert_fusion
  91.1 1.9 all_gather.23
  93.0 0.7 gather_fusion.1
  93.8 2.1 fusion.4
  95.9 7.1 %scatter_fusion.1 = f32[17,64,128]{2,1,0:T(8,128)S(1)} fusion(f32[17,64,128]{2,1,0:T(8,128)S(1)} %broadcast.70.clone, s32[64]{0:T(128)S(1)} %get-tuple-element.9, f32[64,64,128]{2,1,0:T(8,128)} %fusion.4), kind=kCustom, calls=%fused_computation.5 | custom fusion | flops 524288 | bytes 6291712 | tf_op jit(solution)/shard_map/scatter-add | solution.py:64
  103.0 77.5 %all-reduce.1 = bf16[64,2048]{1,0:T(8,128)(2,1)S(1)} all-reduce(f32[64,2048]{1,0:T(8,128)S(1)} %copy_bitcast_fusion.1), channel_id=1, replica_groups=mesh['cell'=16,'gene'=2] {'cell'}, use_global_device_ids=true, to_apply=%region_6.11 | all-reduce | flops 131072 | bytes 786432 | tf_op jit(solution)/shard_map/psum | solution.py:73
  180.5 0.1 copy_bitcast_fusion.4
  180.6 0.8 gather_fusion.2
  181.3 2.9 fusion.2
  184.3 7.1 %scatter_fusion.2 = f32[9,64,128]{2,1,0:T(8,128)S(1)} fusion(f32[9,64,128]{2,1,0:T(8,128)S(1)} %broadcast.69, s32[64]{0:T(128)S(1)} %get-tuple-element.8, f32[64,64,128]{2,1,0:T(8,128)} %fusion.2), kind=kCustom, calls=%fused_computation.6 | custom fusion | flops 524288 | bytes 6291712 | tf_op jit(solution)/shard_map/scatter-add | solution.py:56
  191.3 0.7 copy_bitcast_fusion.2
  192.0 0.0 reduce-scatter.6.cloned.1.call-update
  192.1 0.0 reduce-scatter.8.cloned.1.call-start
  192.1 5.9 %reduce-scatter.6.cloned.1.call-done = f32[64,512]{1,0:T(8,128)} async-done(((f32[64,1024]{1,0:T(8,128)}), f32[64,512]{1,0:T(8,128)}) %reduce-scatter.6.cloned.1.call-update) | async-done | bytes 131088 | tf_op jit(solution)/shard_map/reduce_scatter | solution.py:49
  198.0 0.0 copy-start.2
  198.0 1.3 fusion.41
  199.3 44.7 %all-gather.1 = f32[2048,64]{1,0:T(8,128)S(1)} all-gather(f32[64,64]{1,0:T(8,128)S(1)} %fusion.41), channel_id=3, replica_groups=mesh['cell'=16,'gene'=2] {'cell','gene'}, dimensions={0}, use_global_device_ids=true | all-gather | bytes 540672 | tf_op jit(solution)/shard_map/all_gather | solution.py:43
  244.0 0.1 reduce_sum.19
  244.1 0.1 copy.30
  244.2 5.8 %cholesky.55 = f32[64,64]{1,0:T(8,128)S(1)} custom-call(f32[64,64]{1,0:T(8,128)S(1)} %fusion.28), custom_call_target="Cholesky" | custom-call | tf_op jit(solution)/shard_map/jit(cholesky)/cholesky | solution.py:21
  250.0 0.6 compare_reduce_fusion
  250.7 0.7 fusion.25
  251.4 4.9 %custom-call.7 = f32[1,64,64]{1,2,0:T(8,128)S(1)} custom-call(f32[1,64,64]{2,1,0:T(8,128)S(1)} %fusion.25), custom_call_target="InvertDiagBlocksLowerTriangular" | custom-call | tf_op jit(solution)/shard_map/triangular_solve/custom-call.0 | solution.py:10
  256.2 0.0 copy-done.2
  256.3 0.3 fusion.39
  256.6 1.9 all_gather.27
  258.5 0.7 gather_fusion.3
  259.3 2.1 fusion
  261.4 7.1 %scatter_fusion.3 = f32[17,64,128]{2,1,0:T(8,128)S(1)} fusion(f32[17,64,128]{2,1,0:T(8,128)S(1)} %broadcast.70, s32[64]{0:T(128)S(1)} %get-tuple-element.9, f32[64,64,128]{2,1,0:T(8,128)} %fusion), kind=kCustom, calls=%fused_computation.7 | custom fusion | flops 524288 | bytes 6291712 | tf_op jit(solution)/shard_map/scatter-add | solution.py:64
  268.5 0.8 copy_bitcast_fusion
  269.3 0.0 reduce-scatter.8.cloned.1.call-update
  269.3 1.9 all_gather.26
  271.2 71.8 %reduce-scatter.8.cloned.1.call-done = f32[64,128]{1,0:T(8,128)} async-done(((f32[64,2048]{1,0:T(8,128)}), f32[64,128]{1,0:T(8,128)}) %reduce-scatter.8.cloned.1.call-update) | async-done | bytes 32784 | tf_op jit(solution)/shard_map/reduce_scatter | solution.py:82
  343.1 0.7 copy.59
  (16 shorter events, 0.3 us)
Async XLA Ops:
  7.2 4.0 %copy-start = (bf16[1,64,128,128]{3,2,1,0:T(8,128)(2,1)S(1)}, bf16[1,64,128,128]{3,2,1,0:T(8,128)(2,1)}, u32[]{:S(2)}) copy-start(bf16[1,64,128,128]{3,2,1,0:T(8,128)(2,1)} %param.12) | copy-start | bytes 6291460
  7.2 4.0 %copy-start.3 = (s32[1,64]{1,0:T(1,128)S(1)}, s32[1,64]{1,0:T(1,128)}, u32[]{:S(2)}) copy-start(s32[1,64]{1,0:T(1,128)} %param.14) | copy-start | bytes 772
  7.2 4.0 %copy-start.4 = (s32[1,64]{1,0:T(1,128)S(1)}, s32[1,64]{1,0:T(1,128)}, u32[]{:S(2)}) copy-start(s32[1,64]{1,0:T(1,128)} %param.13) | copy-start | bytes 772
  7.2 25.3 %reduce-scatter.4.cloned.1.call-start = ((), (), s32[]{:S(2)}) async-start(), calls=%async_computation.3 | async-start | bytes 393216 | tf_op jit(solution)/shard_map/reduce_scatter | solution.py:49
  21.9 176.1 %reduce-scatter.6.cloned.1.call-start = ((), (), s32[]{:S(2)}) async-start(), calls=%async_computation.4 | async-start | bytes 393216 | tf_op jit(solution)/shard_map/reduce_scatter | solution.py:49
  32.5 58.3 %copy-start.1 = (f32[64,512]{1,0:T(8,128)S(1)}, f32[64,512]{1,0:T(8,128)}, u32[]{:S(2)}) copy-start(f32[64,512]{1,0:T(8,128)} %reduce-scatter.4.cloned.1.call-done) | copy-start | bytes 393220
  192.1 151.0 %reduce-scatter.8.cloned.1.call-start = ((), (), s32[]{:S(2)}) async-start(), calls=%async_computation.5 | async-start | bytes 557056 | tf_op jit(solution)/shard_map/reduce_scatter | solution.py:82
  198.0 58.3 %copy-start.2 = (f32[64,512]{1,0:T(8,128)S(1)}, f32[64,512]{1,0:T(8,128)}, u32[]{:S(2)}) copy-start(f32[64,512]{1,0:T(8,128)} %reduce-scatter.6.cloned.1.call-done) | copy-start | bytes 393220
Sparse Core Ops, SparseCore 0:
  22.0 10.4 reduce-scatter.3
  192.2 5.7 reduce-scatter.5
  269.5 73.5 reduce-scatter.7
